TPU v7x, 32 devices: a whole 2x2x4 slice. The times are simulated.
32 devices in a mesh: rows: 8 (over z, y), grp: 4 (over x, core).
Axes of the slice: x: 2, y: 2, z: 4, core: 2. Of those that a mesh axis runs over, the one named last changes fastest.
Arguments:
- activations: bfloat16 [3072, 2048], P(('rows', 'grp')), may hold values from 0 to 1
- weight_tiles: bfloat16 [3, 512, 2, 128, 128], P(None, ('rows', 'grp')), may hold values from -0.75 to 0.75
- tile_index: int32 [3, 512, 1], replicated, may hold values from 0 to 511, as said below
- bias_terms: float32 [3, 65536], replicated, may hold values from -0.3 to 0.3
- demand: int32 [32, 16], P(('rows', 'grp')), may hold values from 0 to 511, as said below
Outputs:
- final_acts: bfloat16 [3072, 2048], P(('rows', 'grp'))
Inputs may be any that keep to these rules, and one draw needn't show every extreme that they name: Each row of demand lists 16 distinct blocks made of whole groups [g * 4, (g + 1) * 4); every range [r * 64, (r + 1) * 64) holds either none of them or exactly one group of 4. tile_index[l, b, k] is a block of b's own group [(b // 4) * 4, (b // 4 + 1) * 4), never b itself.
All inputs are finite; a program needn't handle non-finite values.
Results may differ from a plain program's by a relative error of at most 0.0057.
Values may be sent and summed in bfloat16 or wider, within the bound.
A program may use at most 128 MiB of HBM per device.

v0:
```python
import jax
import jax.numpy as jnp
from jax import lax
from jax.sharding import PartitionSpec as P

LAYERS = 3
CAP = 4


def group_step(state, weights, matches, bias_rows):
    chosen = jnp.einsum(
        "sckp,srpt->srckt", matches, state, preferred_element_type=jnp.float32
    ).astype(jnp.bfloat16)
    diag_part = jnp.einsum(
        "srct,sctu->srcu", state, weights[:, :, 0], preferred_element_type=jnp.float32
    )
    off_part = jnp.einsum(
        "srckt,scktu->srcu", chosen, weights[:, :, 1:], preferred_element_type=jnp.float32
    )
    return jax.nn.relu(diag_part + off_part + bias_rows[:, None]).astype(jnp.bfloat16)


def shards(activations, weight_tiles, tile_index, bias_terms, demand):
    live_blocks = demand[0]
    live_count = live_blocks.shape[0]
    tile_width = weight_tiles.shape[-1]
    row_count = lax.axis_size("rows")
    per_range = weight_tiles.shape[1] * lax.axis_size("grp")
    owners = live_blocks // per_range
    within = live_blocks % per_range
    range_ids = jnp.arange(row_count, dtype=jnp.int32)
    slot_ids = jnp.arange(CAP, dtype=jnp.int32)
    current = activations.reshape(activations.shape[0], live_count, tile_width)
    bias_blocks = bias_terms.reshape(bias_terms.shape[0], -1, tile_width)
    grouped = lax.all_gather(weight_tiles, "grp", axis=1, tiled=True)
    member = live_blocks % CAP
    placing = (owners[None, None, :] == range_ids[:, None, None]) & (
        member[None, None, :] == slot_ids[None, :, None]
    )
    starts = jnp.sum(placing[:, 0, :].astype(jnp.int32) * (within[None, :] + 1), axis=1) - 1
    outgoing = jnp.einsum(
        "acp,rpt->arct", placing.astype(jnp.bfloat16), current, preferred_element_type=jnp.float32
    ).astype(jnp.bfloat16)
    arrived = lax.all_to_all(outgoing, "rows", split_axis=0, concat_axis=0, tiled=True)
    bases = lax.all_to_all(
        starts.reshape(row_count, 1), "rows", split_axis=0, concat_axis=0, tiled=True
    )[:, 0]
    slot_blocks = jnp.clip(bases, 0)[:, None] + slot_ids[None, :]
    global_blocks = lax.axis_index("rows") * per_range + slot_blocks
    state = arrived
    for layer_num in range(LAYERS):
        weights = grouped[layer_num][slot_blocks]
        off_member = tile_index[layer_num][global_blocks] % CAP
        matches = (off_member[:, :, :, None] == slot_ids[None, None, None, :]).astype(jnp.bfloat16)
        state = group_step(state, weights, matches, bias_blocks[layer_num][global_blocks])
    returned = lax.all_to_all(state, "rows", split_axis=0, concat_axis=0, tiled=True)
    current = jnp.einsum(
        "acp,arct->rpt", placing.astype(jnp.bfloat16), returned, preferred_element_type=jnp.float32
    ).astype(jnp.bfloat16)
    return current.reshape(current.shape[0], live_count * tile_width)


def solution(mesh):
    return jax.shard_map(
        shards,
        mesh=mesh,
        in_specs=(
            P(("rows", "grp"), None),
            P(None, ("rows", "grp"), None, None, None),
            P(),
            P(),
            P(("rows", "grp"), None),
        ),
        out_specs=P(("rows", "grp"), None),
        check_vma=False,
    )
```

profile of v0, /device:TPU:0, one launch (start us, length us, event | category | flops | bytes accessed | tf_op | source)
XLA Modules:
  0.0 155.7 jit_solution(7514771743446675163)
XLA Ops:
  6.5 0.7 all-gather.2.cloned.1.call-update
  7.5 0.7 copy.36
  8.2 7.3 %all-to-all-start = ((s32[8,1,1]{2,1,0:T(1,128)}), s32[8,1,1]{2,1,0:T(1,128)S(1)}, u32[]{:S(2)}, u32[]{:S(2)}) async-start(s32[8,1,1]{2,1,0:T(1,128)} %copy.36), calls=%async_computation | async-start | bytes 8192 | tf_op jit(solution)/shard_map/all_to_all | solution.py:45
  15.9 1.1 copy.40
  17.0 0.5 fusion.41
  17.5 4.3 %all-to-all-done = s32[8,1,1]{2,1,0:T(1,128)S(1)} async-done(((s32[8,1,1]{2,1,0:T(1,128)}), s32[8,1,1]{2,1,0:T(1,128)S(1)}, u32[]{:S(2)}, u32[]{:S(2)}) %all-to-all-start) | async-done | bytes 64 | tf_op jit(solution)/shard_map/all_to_all | solution.py:45
  21.9 3.6 %all-to-all-start.1 = ((bf16[8,96,4,128]{3,1,2,0:T(8,128)(2,1)}), bf16[8,96,4,128]{3,1,2,0:T(8,128)(2,1)S(1)}, u32[]{:S(2)}, u32[]{:S(2)}) async-start(bf16[8,96,4,128]{3,1,2,0:T(8,128)(2,1)} %copy.40), calls=%async_computation.1 | async-start | bytes 1572864 | tf_op jit(solution)/shard_map/all_to_all | solution.py:44
  26.0 0.7 gather_fusion.7
  26.7 0.7 gather_fusion.5
  27.4 0.7 gather_fusion.3
  28.4 0.6 gather_fusion.8
  29.0 0.6 gather_fusion.4
  29.5 0.6 gather_fusion.6
  30.2 14.3 %all-to-all-done.1 = bf16[8,96,4,128]{3,1,2,0:T(8,128)(2,1)S(1)} async-done(((bf16[8,96,4,128]{3,1,2,0:T(8,128)(2,1)}), bf16[8,96,4,128]{3,1,2,0:T(8,128)(2,1)S(1)}, u32[]{:S(2)}, u32[]{:S(2)}) %all-to-all-start.1) | async-done | bytes 786464 | tf_op jit(solution)/shard_map/all_to_all | solution.py:44
  44.5 1.6 %fusion = bf16[8,96,4,128]{3,2,1,0:T(4,128)(2,1)} fusion(bf16[8,96,4,128]{3,1,2,0:T(8,128)(2,1)S(1)} %all-to-all-done.1, s32[8,4]{1,0:T(8,128)S(1)} %add_select_fusion.2), kind=kOutput, calls=%fused_computation.19 | convolution fusion | flops 3539072 | bytes 1572992 | tf_op jit(solution)/shard_map/sckp,srpt->srckt/dot_general | solution.py:11
  46.1 47.7 %all-gather.2.cloned.1.call-done = bf16[3,64,2,128,128]{4,3,2,1,0:T(8,128)(2,1)} async-done(((bf16[3,16,2,128,128]{4,3,2,1,0:T(8,128)(2,1)}), bf16[3,64,2,128,128]{4,3,2,1,0:T(8,128)(2,1)}) %all-gather.2.cloned.1.call-update) | async-done | bytes 12582928 | tf_op jit(solution)/shard_map/all_gather | solution.py:35
  93.7 8.8 %slice_bitcast_fusion = (bf16[64,2,128,128]{3,2,1,0:T(8,128)(2,1)}, bf16[64,2,128,128]{3,2,1,0:T(8,128)(2,1)}, bf16[64,2,128,128]{3,2,1,0:T(8,128)(2,1)}) fusion(bf16[3,64,2,128,128]{4,3,2,1,0:T(8,128)(2,1)} %all-gather.2.cloned.1.call-done), kind=kLoop, calls=%fused_computation.9 | loop fusion | bytes 25165824 | tf_op jit(solution)/shard_map/squeeze | solution.py:52
  102.6 3.1 %gather_fusion = bf16[32,2,128,128]{3,2,1,0:T(8,128)(2,1)S(1)} fusion(bf16[64,2,128,128]{3,2,1,0:T(8,128)(2,1)} %get-tuple-element.5, s32[1024]{0:T(1024)S(1)} %pad_clamp_fusion.1), kind=kCustom, calls=%fused_computation | custom fusion | bytes 4194432 | tf_op jit(solution)/shard_map/gather | solution.py:52
  105.7 4.3 %gather_fusion.1 = bf16[32,2,128,128]{3,2,1,0:T(8,128)(2,1)} fusion(bf16[64,2,128,128]{3,2,1,0:T(8,128)(2,1)} %get-tuple-element.7, s32[1024]{0:T(1024)S(1)} %pad_clamp_fusion.1), kind=kCustom, calls=%fused_computation.1 | custom fusion | bytes 4194432 | tf_op jit(solution)/shard_map/gather | solution.py:52
  110.0 4.3 %gather_fusion.2 = bf16[32,2,128,128]{3,2,1,0:T(8,128)(2,1)} fusion(bf16[64,2,128,128]{3,2,1,0:T(8,128)(2,1)} %get-tuple-element.6, s32[1024]{0:T(1024)S(1)} %pad_clamp_fusion.1), kind=kCustom, calls=%fused_computation.2 | custom fusion | bytes 4194432 | tf_op jit(solution)/shard_map/gather | solution.py:52
  114.4 1.9 %copy.39 = bf16[32,2,128,128]{3,2,0,1:T(8,128)(2,1)S(1)} copy(bf16[32,2,128,128]{3,2,1,0:T(8,128)(2,1)} %gather_fusion.2) | data formatting | bytes 4194304 | tf_op jit(solution)/shard_map/gather | solution.py:52
  117.4 0.7 copy-done.1
  118.1 0.5 fusion.4
  118.6 0.6 fusion.1
  119.2 0.4 fusion.9
  119.6 0.5 fusion.5
  120.1 0.6 fusion.2
  120.7 0.4 fusion.8
  121.2 0.5 fusion.6
  121.6 25.8 %all_to_all.16 = bf16[8,96,4,128]{3,1,2,0:T(8,128)(2,1)S(1)} all-to-all(bf16[8,96,4,128]{3,1,2,0:T(8,128)(2,1)S(1)} %fusion.6), channel_id=1, replica_groups=mesh['rows'=8,'grp'=4] {'rows'}, dimensions={0} | all-to-all | bytes 1572864 | tf_op jit(solution)/shard_map/all_to_all | solution.py:56
  147.5 0.5 fusion.7
  148.0 0.9 copy.70
  (37 shorter events, 2.5 us)
Async XLA Ops:
  6.5 0.7 copy-start.5
  6.5 8.9 %copy-start.3 = (bf16[96,2048]{1,0:T(8,128)(2,1)S(1)}, bf16[96,2048]{1,0:T(8,128)(2,1)}, u32[]{:S(2)}) copy-start(bf16[96,2048]{1,0:T(8,128)(2,1)} %param.5) | copy-start | bytes 1179652
  6.5 87.2 %all-gather.2.cloned.1.call-start = ((), (), s32[]{:S(2)}) async-start(), calls=%async_computation.3 | async-start | bytes 15728640 | tf_op jit(solution)/shard_map/all_gather | solution.py:35
  7.3 9.7 %copy-start.2 = (f32[3,65536]{1,0:T(4,128)S(1)}, f32[3,65536]{1,0:T(4,128)}, u32[]{:S(2)}) copy-start(f32[3,65536]{1,0:T(4,128)} %param.8) | copy-start | bytes 2359300
  8.2 13.7 %all-to-all-start = ((s32[8,1,1]{2,1,0:T(1,128)}), s32[8,1,1]{2,1,0:T(1,128)S(1)}, u32[]{:S(2)}, u32[]{:S(2)}) async-start(s32[8,1,1]{2,1,0:T(1,128)} %copy.36), calls=%async_computation | async-start | bytes 8192 | tf_op jit(solution)/shard_map/all_to_all | solution.py:45
  15.9 9.6 %copy-start.4 = (s32[3,512,1]{1,2,0:T(1,128)S(1)}, s32[3,512,1]{1,2,0:T(1,128)}, u32[]{:S(2)}) copy-start(s32[3,512,1]{1,2,0:T(1,128)} %param.7) | copy-start | bytes 18436
  21.9 22.6 %all-to-all-start.1 = ((bf16[8,96,4,128]{3,1,2,0:T(8,128)(2,1)}), bf16[8,96,4,128]{3,1,2,0:T(8,128)(2,1)S(1)}, u32[]{:S(2)}, u32[]{:S(2)}) async-start(bf16[8,96,4,128]{3,1,2,0:T(8,128)(2,1)} %copy.40), calls=%async_computation.1 | async-start | bytes 1572864 | tf_op jit(solution)/shard_map/all_to_all | solution.py:44
  114.4 2.2 %copy-start = (bf16[32,2,128,128]{3,2,1,0:T(8,128)(2,1)S(1)}, bf16[32,2,128,128]{3,2,1,0:T(8,128)(2,1)}, u32[]{:S(2)}) copy-start(bf16[32,2,128,128]{3,2,1,0:T(8,128)(2,1)} %gather_fusion.1) | copy-start | bytes 6291460
  117.0 1.1 copy-start.1
Sparse Core Ops, SparseCore 0:
  8.9 84.7 all-gather.1
where the time goes:
time: 156 us
  waiting for transfers between devices  67 us (43%)
  local copies, waits for them, and re-layouts  31.4 us (20%)
  blocking collectives  25.8 us (17%)
  between operations  13.6 us (9%)
  starting transfers between devices  10.9 us (7%)
  matrix products  6.37 us (4%)
    all_gather x1, waiting for transfers between devices, shards(): grouped = lax.all_gather(weight_tiles, 'grp', axis=1, tiled=True)  47.7 us
    all_to_all x1, blocking collectives, shards(): lax.all_to_all(state, 'rows', split_axis=0, concat_axis=0, tiled=True)  25.8 us
    all_to_all x1, waiting for transfers between devices, shards(): lax.all_to_all(outgoing, 'rows', split_axis=0, concat_axis=0, tiled=True)  14.3 us
    gather x6, local copies, waits for them, and re-layouts, shards(): weights = grouped[layer_num][slot_blocks]  14 us
    squeeze x1, local copies, waits for them, and re-layouts, shards(): weights = grouped[layer_num][slot_blocks]  8.84 us
    all_to_all x1, starting transfers between devices, shards(): lax.all_to_all(starts.reshape(row_count, 1), 'rows', split_axis=0, concat...  7.31 us
    all_to_all x1, waiting for transfers between devices, shards(): lax.all_to_all(starts.reshape(row_count, 1), 'rows', split_axis=0, concat...  4.33 us
    all_to_all x1, starting transfers between devices, shards(): lax.all_to_all(outgoing, 'rows', split_axis=0, concat_axis=0, tiled=True)  3.59 us
  transfers between devices with their start and end apart: 3, of which 3 were waited for; matrix products, arithmetic and copies ran while one was open for 6% of the time, Pallas kernels for 0%

commit v1 on v0

--- a/solution.py
+++ b/solution.py
@@ -1,10 +1,17 @@
+import functools
+
 import jax
 import jax.numpy as jnp
 from jax import lax
+from jax.experimental import pallas as pl
+from jax.experimental.pallas import tpu as pltpu
 from jax.sharding import PartitionSpec as P
 
-LAYERS = 3
 CAP = 4
+CORES = 2
+PLANES = 2
+LAG = 3
+MESH = pl.DeviceIdType.MESH
 
 
 def group_step(state, weights, matches, bias_rows):
@@ -20,7 +27,7 @@
     return jax.nn.relu(diag_part + off_part + bias_rows[:, None]).astype(jnp.bfloat16)
 
 
-def shards(activations, weight_tiles, tile_index, bias_terms, demand):
+def gathered_shards(activations, weight_tiles, tile_index, bias_terms, demand):
     live_blocks = demand[0]
     live_count = live_blocks.shape[0]
     tile_width = weight_tiles.shape[-1]
@@ -48,7 +55,7 @@
     slot_blocks = jnp.clip(bases, 0)[:, None] + slot_ids[None, :]
     global_blocks = lax.axis_index("rows") * per_range + slot_blocks
     state = arrived
-    for layer_num in range(LAYERS):
+    for layer_num in range(weight_tiles.shape[0]):
         weights = grouped[layer_num][slot_blocks]
         off_member = tile_index[layer_num][global_blocks] % CAP
         matches = (off_member[:, :, :, None] == slot_ids[None, None, None, :]).astype(jnp.bfloat16)
@@ -60,7 +67,284 @@
     return current.reshape(current.shape[0], live_count * tile_width)
 
 
+def fused_kernel(
+    n, pos_ref, home_ref, index_ref, meta_ref, act_ref, bias_ref, w_hbm, out_ref,
+    w_all, slots, zin, xin, ores, fres, xres, sel, fin, st_own, st_for, meta_in, meta_s,
+    w_sems, m_send, m_recv, m_copy, z_send, z_recv, x_send, x_recv,
+    b_send, b_recv, f_send, f_recv,
+):
+    layers, held = w_hbm.shape[0], w_hbm.shape[1]
+    tile = w_hbm.shape[-1]
+    live = home_ref.shape[1]
+    r = lax.axis_index("rows")
+    g = lax.axis_index("grp")
+    plane, core = g // CORES, g % CORES
+    mate = plane * CORES + (CORES - 1 - core)
+    cross = (PLANES - 1 - plane) * CORES + core
+
+    def up(k):
+        return lax.rem(r + k, n)
+
+    def down(k):
+        return lax.rem(r - k + n, n)
+
+    barrier = pltpu.get_barrier_semaphore()
+    pl.semaphore_signal(barrier, inc=1, device_id=(r, mate), device_id_type=MESH)
+
+    def greet(k, carry):
+        pl.semaphore_signal(barrier, inc=1, device_id=(up(k), g), device_id_type=MESH)
+        pl.semaphore_signal(barrier, inc=1, device_id=(up(k), cross), device_id_type=MESH)
+        return carry
+
+    lax.fori_loop(1, n, greet, 0)
+    pl.semaphore_signal(barrier, inc=1, device_id=(r, cross), device_id_type=MESH)
+
+    w_local = pltpu.make_async_copy(w_hbm, w_all.at[core], w_sems.at[0])
+    w_local.start()
+    for a in range(n):
+        for c in range(CAP):
+            slots[a, c] = act_ref[pos_ref[a, c]]
+    meta_in[0, r] = meta_ref[r]
+    pl.semaphore_wait(barrier, 2 * n)
+
+    def meta_copy(which, slot, row, dev_row, dev_grp):
+        return pltpu.make_async_remote_copy(
+            src_ref=meta_ref.at[row], dst_ref=meta_in.at[which, slot],
+            send_sem=m_send.at[which, row], recv_sem=m_recv.at[which, slot],
+            device_id=(dev_row, dev_grp), device_id_type=MESH,
+        )
+
+    def z_copy(row, slot):
+        return pltpu.make_async_remote_copy(
+            src_ref=slots.at[row], dst_ref=zin.at[slot],
+            send_sem=z_send.at[row], recv_sem=z_recv.at[slot],
+            device_id=(row, g), device_id_type=MESH,
+        )
+
+    def x_copy(src, slot):
+        return pltpu.make_async_remote_copy(
+            src_ref=src.at[slot], dst_ref=xin.at[slot],
+            send_sem=x_send.at[slot], recv_sem=x_recv.at[slot],
+            device_id=(r, cross), device_id_type=MESH,
+        )
+
+    def b_copy(slot):
+        return pltpu.make_async_remote_copy(
+            src_ref=fres.at[slot], dst_ref=xres.at[slot],
+            send_sem=b_send.at[slot], recv_sem=b_recv.at[slot],
+            device_id=(r, cross), device_id_type=MESH,
+        )
+
+    def f_copy(row, slot):
+        return pltpu.make_async_remote_copy(
+            src_ref=sel.at[row], dst_ref=fin.at[slot],
+            send_sem=f_send.at[row], recv_sem=f_recv.at[slot],
+            device_id=(row, g), device_id_type=MESH,
+        )
+
+    w_remote = pltpu.make_async_remote_copy(
+        src_ref=w_hbm, dst_ref=w_all.at[core],
+        send_sem=w_sems.at[1], recv_sem=w_sems.at[2],
+        device_id=(r, mate), device_id_type=MESH,
+    )
+    w_arrives = pltpu.make_async_remote_copy(
+        src_ref=w_hbm, dst_ref=w_all.at[CORES - 1 - core],
+        send_sem=w_sems.at[1], recv_sem=w_sems.at[2],
+        device_id=(r, mate), device_id_type=MESH,
+    )
+
+    def send_meta(k, carry):
+        row = up(k)
+        meta_copy(0, r, row, row, g).start()
+        meta_copy(1, r, row, row, cross).start()
+        return carry
+
+    x_copy(slots, r).start()
+    meta_copy(1, r, r, r, cross).start()
+    lax.fori_loop(1, n, send_meta, 0)
+
+    def send_rows(k, carry):
+        z_copy(up(k), r).start()
+        return carry
+
+    lax.fori_loop(1, n, send_rows, 0)
+    w_remote.start()
+
+    def forward(k):
+        slot = down(k)
+        z_copy(r, slot).wait_recv()
+        x_copy(zin, slot).start()
+
+    for k in range(1, min(LAG, n)):
+        forward(k)
+    meta_copy(1, r, r, r, cross).wait_recv()
+
+    def take_meta(k, carry):
+        meta_copy(0, down(k), r, r, g).wait_recv()
+        meta_copy(1, down(k), r, r, cross).wait_recv()
+        return carry
+
+    lax.fori_loop(1, n, take_meta, 0)
+    to_smem = pltpu.make_async_copy(meta_in, meta_s, m_copy)
+    to_smem.start()
+    to_smem.wait()
+    w_local.wait()
+    w_arrives.wait_recv()
+
+    def compute(jobs):
+        for load, slot, _, state, _ in jobs:
+            for j in range(CAP):
+                state[0, j] = load[slot, j]
+        for layer in range(layers):
+            for _, slot, store, state, which in jobs:
+                half = meta_s[which, slot, 0, 0]
+                local = meta_s[which, slot, 0, 1]
+                inner = meta_s[which, slot, 0, 2]
+                for j in range(CAP):
+                    other = index_ref[layer, inner + j]
+                    pair = (state[layer % 2, j], state[layer % 2, other])
+                    pre = jnp.dot(
+                        jnp.concatenate(pair, axis=1), w_all[half, layer, local + j],
+                        preferred_element_type=jnp.float32,
+                    ) + bias_ref[layer, inner + j]
+                    value = jnp.maximum(pre, 0.0).astype(jnp.bfloat16)
+                    if layer == layers - 1:
+                        store[slot, j] = value
+                    else:
+                        state[(layer + 1) % 2, j] = value
+
+    def step(k, own_buf):
+        slot = down(k)
+        x_copy(zin, slot).wait_recv()
+        compute((
+            (xin, slot, fres, st_for, 1),
+            (own_buf, slot, ores, st_own, 0),
+        ))
+        b_copy(slot).start()
+
+    def choose(slot):
+        b_copy(slot).wait_recv()
+        mine = (meta_s[0, slot, 0, 3] == plane).astype(jnp.float32)
+        for j in range(CAP):
+            sel[slot, j] = (
+                ores[slot, j].astype(jnp.float32) * mine
+                + xres[slot, j].astype(jnp.float32) * (1.0 - mine)
+            ).astype(jnp.bfloat16)
+
+    if LAG < n:
+        forward(LAG)
+    step(0, slots)
+
+    def early(k, carry):
+        forward(k + LAG)
+        step(k, zin)
+        return carry
+
+    lax.fori_loop(1, n - LAG, early, 0)
+    choose(r)
+
+    def late(k, carry):
+        step(k, zin)
+        slot = down(k - (n - LAG) + 1)
+        choose(slot)
+        f_copy(slot, r).start()
+        return carry
+
+    lax.fori_loop(n - LAG, n, late, 0)
+
+    def last(k, carry):
+        slot = down(k)
+        choose(slot)
+        f_copy(slot, r).start()
+        return carry
+
+    lax.fori_loop(LAG + 1, n, last, 0)
+
+    def take(k, carry):
+        f_copy(r, down(k)).wait_recv()
+        return carry
+
+    lax.fori_loop(1, n, take, 0)
+    fin[r] = sel[r]
+    for p in range(live):
+        out_ref[:, p * tile:(p + 1) * tile] = fin[home_ref[0, p], home_ref[1, p]]
+
+    def drain(k, carry):
+        row = up(k)
+        meta_copy(0, r, row, row, g).wait_send()
+        meta_copy(1, r, row, row, cross).wait_send()
+        z_copy(row, r).wait_send()
+        x_copy(zin, row).wait_send()
+        b_copy(row).wait_send()
+        f_copy(row, r).wait_send()
+        return carry
+
+    lax.fori_loop(1, n, drain, 0)
+    meta_copy(1, r, r, r, cross).wait_send()
+    x_copy(slots, r).wait_send()
+    b_copy(r).wait_send()
+    w_remote.wait_send()
+
+
+def fused_shards(activations, weight_tiles, tile_index, bias_terms, demand):
+    n = lax.axis_size("rows")
+    layers, held, kinds, tile, _ = weight_tiles.shape
+    per_range = held * lax.axis_size("grp")
+    depth = activations.shape[0]
+    blocks = demand[0]
+    owners, within, member = blocks // per_range, blocks % per_range, blocks % CAP
+    placing = (owners[None, None, :] == jnp.arange(n, dtype=jnp.int32)[:, None, None]) & (
+        member[None, None, :] == jnp.arange(CAP, dtype=jnp.int32)[None, :, None]
+    )
+    places = jnp.arange(blocks.shape[0], dtype=jnp.int32)
+    pos = jnp.sum(jnp.where(placing, places, 0), axis=2)
+    starts = jnp.sum(jnp.where(placing[:, 0], within, 0), axis=1)
+    chip_blocks = held * CORES
+    inner = starts % chip_blocks
+    facts = jnp.stack([inner // held, inner % held, inner, starts // chip_blocks], axis=1)
+    meta = jnp.pad(facts, ((0, 0), (0, 124)))[:, None, :]
+    home = jnp.stack([owners, member])
+    chip = (lax.axis_index("rows") * PLANES + lax.axis_index("grp") // CORES) * chip_blocks
+    others = lax.dynamic_slice_in_dim(tile_index[:, :, 0], chip, chip_blocks, axis=1) % CAP
+    bias = lax.dynamic_slice_in_dim(bias_terms, chip * tile, chip_blocks * tile, axis=1)
+    bias = bias.reshape(layers, chip_blocks, 1, tile)
+    weights = weight_tiles.reshape(layers, held, kinds * tile, tile)
+    columns = activations.reshape(depth, blocks.shape[0], tile).transpose(1, 0, 2)
+    smem = pl.BlockSpec(memory_space=pltpu.SMEM)
+    vmem = pl.BlockSpec(memory_space=pltpu.VMEM)
+    slot = pltpu.VMEM((n, CAP, depth, tile), jnp.bfloat16)
+    sems = pltpu.SemaphoreType.DMA((n,))
+    return pl.pallas_call(
+        functools.partial(fused_kernel, n),
+        out_shape=jax.ShapeDtypeStruct(activations.shape, jnp.bfloat16),
+        in_specs=[smem, smem, smem, vmem, vmem, vmem, pl.BlockSpec(memory_space=pl.ANY)],
+        out_specs=vmem,
+        scratch_shapes=[
+            pltpu.VMEM((CORES, layers, held, kinds * tile, tile), jnp.bfloat16),
+            slot, slot, slot, slot, slot, slot, slot, slot,
+            pltpu.VMEM((2, CAP, depth, tile), jnp.bfloat16),
+            pltpu.VMEM((2, CAP, depth, tile), jnp.bfloat16),
+            pltpu.VMEM((2, n, 1, 128), jnp.int32),
+            pltpu.SMEM((2, n, 1, 128), jnp.int32),
+            pltpu.SemaphoreType.DMA((3,)),
+            pltpu.SemaphoreType.DMA((2, n)),
+            pltpu.SemaphoreType.DMA((2, n)),
+            pltpu.SemaphoreType.DMA,
+            sems, sems, sems, sems, sems, sems, sems, sems,
+        ],
+        compiler_params=pltpu.CompilerParams(
+            collective_id=0, has_side_effects=True, vmem_limit_bytes=40 * 1024 * 1024
+        ),
+    )(pos, home, others, meta, columns, bias, weights)
+
+
 def solution(mesh):
+    def shards(activations, weight_tiles, tile_index, bias_terms, demand):
+        whole_groups = weight_tiles.shape[1] % CAP == 0 and weight_tiles.shape[2] == 2
+        if whole_groups and mesh.shape["grp"] == PLANES * CORES and mesh.shape["rows"] > 2 * LAG:
+            return fused_shards(activations, weight_tiles, tile_index, bias_terms, demand)
+        return gathered_shards(activations, weight_tiles, tile_index, bias_terms, demand)
+
     return jax.shard_map(
         shards,
         mesh=mesh,

time: 156 us -> 65.8 us (0.42)
  waiting for transfers between devices: 67 us -> 0 us
  Pallas kernels: 0 us -> 59 us
  local copies, waits for them, and re-layouts: 31.4 us -> 4.81 us
  blocking collectives: 25.8 us -> 0 us
  between operations: 13.6 us -> 0.06 us
  starting transfers between devices: 10.9 us -> 0 us
  matrix products: 6.37 us -> 0 us
    pallas_call x0 -> x1, Pallas kernels: none -> 59 us  [fused_shards(): pl.pallas_call(functools.partial(fused_kernel, n), out_shape=jax.ShapeDty...]
    all_gather x1 -> x0, waiting for transfers between devices: 47.7 us -> none  [shards(): grouped = lax.all_gather(weight_tiles, 'grp', axis=1, tiled=True)]
    all_to_all x1 -> x0, blocking collectives: 25.8 us -> none  [shards(): lax.all_to_all(state, 'rows', split_axis=0, concat_axis=0, tiled=True)]
    all_to_all x2 -> x0, waiting for transfers between devices: 18.7 us -> none  [the longest x1 14.3 us: shards(): lax.all_to_all(outgoing, 'rows', split_axis=0, concat_axis=0, tiled=True)]
    gather x15 -> x0, local copies, waits for them, and re-layouts: 18.1 us -> none  [the longest x6 14 us: shards(): weights = grouped[layer_num][slot_blocks]]
    all_to_all x2 -> x0, starting transfers between devices: 10.9 us -> none  [the longest x1 7.31 us: shards(): lax.all_to_all(starts.reshape(row_count, 1), 'rows', split_axis=0, concat...]
    squeeze x1 -> x0, local copies, waits for them, and re-layouts: 8.84 us -> none  [shards(): weights = grouped[layer_num][slot_blocks]]
    dot_general x11 -> x0, matrix products: 6.37 us -> none  [the longest x3 2.82 us: group_step(): jnp.einsum('sckp,srpt->srckt', matches, state, preferred_element_type=jnp...]
  transfers between devices with their start and end apart: 3 -> 0, of which waited for: 3 -> 0; matrix products, arithmetic and copies ran while one was open for 6% -> 0% of each run, Pallas kernels for 0% -> 0%
where the time goes in v1:
time: 65.8 us; the launch traced here: 65.6 us
  Pallas kernels  59 us (90%)
  local copies, waits for them, and re-layouts  4.81 us (7%)
  other arithmetic  1.74 us (3%)
    pallas_call x1, Pallas kernels, fused_shards(): pl.pallas_call(functools.partial(fused_kernel, n), out_shape=jax.ShapeDty...  59 us
    unnamed x5, local copies, waits for them, and re-layouts  2.64 us

profile of v1, /device:TPU:0, one launch (start us, length us, event | category | flops | bytes accessed | tf_op | source)
XLA Modules:
  0.0 65.6 jit_solution(14370063311288550837)
XLA Ops:
  0.0 0.0 copy-start
  0.0 0.8 %constant_dynamic-slice_fusion.1 = s32[3,32,1]{1,2,0:T(1,128)S(1)} fusion(s32[3,512,1]{1,2,0:T(1,128)} %param.7, s32[]{:T(128)S(6)} %select_n.114), kind=kLoop, calls=%fused_computation.45 | loop fusion | bytes 772 | tf_op jit(solution)/shard_map/dynamic_slice | solution.py:308
  0.9 0.7 %and_select_fusion.2 = (s32[1,16]{1,0:T(1,128)S(1)}, s32[1,16]{1,0:T(1,128)S(1)}) fusion(s32[1,16]{1,0:T(1,128)} %param.9), kind=kLoop, calls=%fused_computation.30 | loop fusion | flops 368 | bytes 192 | tf_op jit(solution)/shard_map/jit(floor_divide)/jit(_where)/select_n | solution.py:295
  1.5 0.7 %and_select_fusion = (s32[16]{0:T(128)S(1)}, s32[16]{0:T(128)S(1)}, s32[16]{0:T(128)S(1)}) fusion(s32[1,16]{1,0:T(1,128)} %param.9), kind=kLoop, calls=%fused_computation.28 | loop fusion | flops 432 | bytes 256 | tf_op jit(solution)/shard_map/jit(remainder)/select_n | solution.py:295
  2.2 0.1 select_reduce_fusion
  2.4 0.1 copy.20.pos_ref
  2.5 0.1 select_reduce_fusion.1
  2.6 0.1 copy.15
  2.7 0.1 pad_add_fusion
  2.8 0.0 copy-done
  2.8 0.1 reshape.250.bias_ref
  2.9 1.1 %bitcast_bitcast_fusion.act_ref = bf16[16,96,128]{2,1,0:T(8,128)(2,1)S(1)} fusion(bf16[96,2048]{1,0:T(8,128)(2,1)} %param.5), kind=kLoop, calls=%fused_computation | loop fusion | bytes 786432 | tf_op jit(solution)/shard_map/transpose | solution.py:312
  4.0 0.0 copy-start.1
  4.0 1.9 %copy-done.1 = bf16[3,16,2,128,128]{4,3,2,1,0:T(8,128)(2,1)S(1)} copy-done((bf16[3,16,2,128,128]{4,3,2,1,0:T(8,128)(2,1)S(1)}, bf16[3,16,2,128,128]{4,3,2,1,0:T(8,128)(2,1)}, u32[]{:S(2)}) %copy-start.1) | copy-done | bytes 3145752
  5.9 59.0 %shard_map.55 = bf16[96,2048]{1,0:T(8,128)(2,1)S(1)} custom-call(s32[8,4]{1,0:T(8,128)S(1)} %copy.20.pos_ref, s32[2,16]{1,0:T(2,128)S(1)} %pad_add_fusion.1.home_ref, s32[3,32]{1,0:T(4,128)S(1)} %add_select_fusion.4.index_ref, s32[8,1,128]{2,1,0:T(1,128)S(1)} %bitcast.43, bf16[16,96,128]{2,1,0:T(8,128)(2,1)S(1)} %bitcast_bitcast_fusion.act_ref, ...), custom_call_target="tpu_custom_call" | custom-call | tf_op jit(solution)/shard_map/pallas_call | solution.py:317
  64.8 0.7 %copy.28 = bf16[96,2048]{1,0:T(8,128)(2,1)} copy(bf16[96,2048]{1,0:T(8,128)(2,1)S(1)} %shard_map.55) | data formatting | bytes 786432
  (8 shorter events, 0.1 us)
Async XLA Ops:
  0.0 2.8 %copy-start = (f32[3,65536]{1,0:T(4,128)S(1)}, f32[3,65536]{1,0:T(4,128)}, u32[]{:S(2)}) copy-start(f32[3,65536]{1,0:T(4,128)} %param.8) | copy-start | bytes 2359300
  4.0 1.9 %copy-start.1 = (bf16[3,16,2,128,128]{4,3,2,1,0:T(8,128)(2,1)S(1)}, bf16[3,16,2,128,128]{4,3,2,1,0:T(8,128)(2,1)}, u32[]{:S(2)}) copy-start(bf16[3,16,2,128,128]{4,3,2,1,0:T(8,128)(2,1)} %param.6) | copy-start | bytes 9437188

commit v2 on v1

--- a/solution.py
+++ b/solution.py
@@ -11,6 +11,7 @@
 CORES = 2
 PLANES = 2
 LAG = 3
+BACK = 2
 MESH = pl.DeviceIdType.MESH
 
 
@@ -231,34 +232,34 @@
                 + xres[slot, j].astype(jnp.float32) * (1.0 - mine)
             ).astype(jnp.bfloat16)
 
-    if LAG < n:
-        forward(LAG)
-    step(0, slots)
-
-    def early(k, carry):
-        forward(k + LAG)
-        step(k, zin)
-        return carry
-
-    lax.fori_loop(1, n - LAG, early, 0)
-    choose(r)
-
-    def late(k, carry):
-        step(k, zin)
-        slot = down(k - (n - LAG) + 1)
-        choose(slot)
-        f_copy(slot, r).start()
-        return carry
-
-    lax.fori_loop(n - LAG, n, late, 0)
-
-    def last(k, carry):
+    def send_back(k, carry):
         slot = down(k)
         choose(slot)
         f_copy(slot, r).start()
         return carry
 
-    lax.fori_loop(LAG + 1, n, last, 0)
+    forward(LAG)
+    step(0, slots)
+
+    def first(k, carry):
+        forward(k + LAG)
+        step(k, zin)
+        return carry
+
+    def middle(k, carry):
+        forward(k + LAG)
+        step(k, zin)
+        return send_back(k - BACK, carry)
+
+    def late(k, carry):
+        step(k, zin)
+        return send_back(k - BACK, carry)
+
+    lax.fori_loop(1, BACK + 1, first, 0)
+    choose(r)
+    lax.fori_loop(BACK + 1, n - LAG, middle, 0)
+    lax.fori_loop(n - LAG, n, late, 0)
+    lax.fori_loop(n - BACK, n, send_back, 0)
 
     def take(k, carry):
         f_copy(r, down(k)).wait_recv()
@@ -341,7 +342,7 @@
 def solution(mesh):
     def shards(activations, weight_tiles, tile_index, bias_terms, demand):
         whole_groups = weight_tiles.shape[1] % CAP == 0 and weight_tiles.shape[2] == 2
-        if whole_groups and mesh.shape["grp"] == PLANES * CORES and mesh.shape["rows"] > 2 * LAG:
+        if whole_groups and mesh.shape["grp"] == PLANES * CORES and mesh.shape["rows"] > LAG + BACK:
             return fused_shards(activations, weight_tiles, tile_index, bias_terms, demand)
         return gathered_shards(activations, weight_tiles, tile_index, bias_terms, demand)
 

time: 65.8 us -> 64 us (0.973)
  Pallas kernels: 59 us -> 57.2 us
    pallas_call x1, Pallas kernels: 59 us -> 57.2 us  [fused_shards(): pl.pallas_call(functools.partial(fused_kernel, n), out_shape=jax.ShapeDty...]
where the time goes in v2:
time: 64 us; the launch traced here: 63.8 us
  Pallas kernels  57.2 us (89%)
  local copies, waits for them, and re-layouts  4.81 us (8%)
  other arithmetic  1.74 us (3%)
    pallas_call x1, Pallas kernels, fused_shards(): pl.pallas_call(functools.partial(fused_kernel, n), out_shape=jax.ShapeDty...  57.2 us
    unnamed x5, local copies, waits for them, and re-layouts  2.64 us

profile of v2, /device:TPU:0, one launch (start us, length us, event | category | flops | bytes accessed | tf_op | source)
XLA Modules:
  0.0 63.8 jit_solution(7080102079083713177)
XLA Ops:
  0.0 0.0 copy-start
  0.0 0.8 %constant_dynamic-slice_fusion.1 = s32[3,32,1]{1,2,0:T(1,128)S(1)} fusion(s32[3,512,1]{1,2,0:T(1,128)} %param.7, s32[]{:T(128)S(6)} %select_n.114), kind=kLoop, calls=%fused_computation.45 | loop fusion | bytes 772 | tf_op jit(solution)/shard_map/dynamic_slice | solution.py:309
  0.9 0.7 %and_select_fusion.2 = (s32[1,16]{1,0:T(1,128)S(1)}, s32[1,16]{1,0:T(1,128)S(1)}) fusion(s32[1,16]{1,0:T(1,128)} %param.9), kind=kLoop, calls=%fused_computation.30 | loop fusion | flops 368 | bytes 192 | tf_op jit(solution)/shard_map/jit(floor_divide)/jit(_where)/select_n | solution.py:296
  1.5 0.7 %and_select_fusion = (s32[16]{0:T(128)S(1)}, s32[16]{0:T(128)S(1)}, s32[16]{0:T(128)S(1)}) fusion(s32[1,16]{1,0:T(1,128)} %param.9), kind=kLoop, calls=%fused_computation.28 | loop fusion | flops 432 | bytes 256 | tf_op jit(solution)/shard_map/jit(remainder)/select_n | solution.py:296
  2.2 0.1 select_reduce_fusion
  2.4 0.1 copy.20.pos_ref
  2.5 0.1 select_reduce_fusion.1
  2.6 0.1 copy.15
  2.7 0.1 pad_add_fusion
  2.8 0.0 copy-done
  2.8 0.1 reshape.250.bias_ref
  2.9 1.1 %bitcast_bitcast_fusion.act_ref = bf16[16,96,128]{2,1,0:T(8,128)(2,1)S(1)} fusion(bf16[96,2048]{1,0:T(8,128)(2,1)} %param.5), kind=kLoop, calls=%fused_computation | loop fusion | bytes 786432 | tf_op jit(solution)/shard_map/transpose | solution.py:313
  4.0 0.0 copy-start.1
  4.0 1.9 %copy-done.1 = bf16[3,16,2,128,128]{4,3,2,1,0:T(8,128)(2,1)S(1)} copy-done((bf16[3,16,2,128,128]{4,3,2,1,0:T(8,128)(2,1)S(1)}, bf16[3,16,2,128,128]{4,3,2,1,0:T(8,128)(2,1)}, u32[]{:S(2)}) %copy-start.1) | copy-done | bytes 3145752
  5.9 57.2 %shard_map.55 = bf16[96,2048]{1,0:T(8,128)(2,1)S(1)} custom-call(s32[8,4]{1,0:T(8,128)S(1)} %copy.20.pos_ref, s32[2,16]{1,0:T(2,128)S(1)} %pad_add_fusion.1.home_ref, s32[3,32]{1,0:T(4,128)S(1)} %add_select_fusion.4.index_ref, s32[8,1,128]{2,1,0:T(1,128)S(1)} %bitcast.43, bf16[16,96,128]{2,1,0:T(8,128)(2,1)S(1)} %bitcast_bitcast_fusion.act_ref, ...), custom_call_target="tpu_custom_call" | custom-call | tf_op jit(solution)/shard_map/pallas_call | solution.py:318
  63.0 0.7 %copy.28 = bf16[96,2048]{1,0:T(8,128)(2,1)} copy(bf16[96,2048]{1,0:T(8,128)(2,1)S(1)} %shard_map.55) | data formatting | bytes 786432
  (8 shorter events, 0.1 us)
Async XLA Ops:
  0.0 2.8 %copy-start = (f32[3,65536]{1,0:T(4,128)S(1)}, f32[3,65536]{1,0:T(4,128)}, u32[]{:S(2)}) copy-start(f32[3,65536]{1,0:T(4,128)} %param.8) | copy-start | bytes 2359300
  4.0 1.9 %copy-start.1 = (bf16[3,16,2,128,128]{4,3,2,1,0:T(8,128)(2,1)S(1)}, bf16[3,16,2,128,128]{4,3,2,1,0:T(8,128)(2,1)}, u32[]{:S(2)}) copy-start(bf16[3,16,2,128,128]{4,3,2,1,0:T(8,128)(2,1)} %param.6) | copy-start | bytes 9437188
